TPU v7x, 32 devices: a whole 2x2x4 slice. The times are simulated.
32 devices in a mesh: band: 8 (over z, y), grid: 4 (over x, core).
Axes of the slice: x: 2, y: 2, z: 4, core: 2. Of those that a mesh axis runs over, the one named last changes fastest.
Arguments:
- orbitals: bfloat16 [8, 128, 128, 128], P('band', 'grid'), may hold values from -3 to 3
- trial_vectors: bfloat16 [2, 8, 128, 128, 128], P(None, 'band', 'grid'), may hold values from -6 to 6
- alda_kernel: float32 [128, 128, 128], P('grid'), may hold values from -2 to -0.5
- local_potential: float32 [128, 128, 128], P('grid'), may hold values from -2 to 1
- band_energies: float32 [8], P('band'), may hold values from -1.5 to -0.2
Outputs:
- sigma_real: float32 [2, 8, 128, 128, 128], P(None, 'band', 'grid')
- sigma_imag: float32 [2, 8, 128, 128, 128], P(None, 'band', 'grid')
All inputs are finite; a program needn't handle non-finite values.
Results may differ from a plain program's by a relative error of at most 0.0003.
Values sent between devices are 32-bit elements; how exact they have to be, the bound alone decides.
A program may use at most 64 MiB of HBM per device.

v0:
```python
import math
import jax
import jax.numpy as jnp
from jax import lax
from jax.sharding import PartitionSpec as P

box_length = 30.0
highest = lax.Precision.HIGHEST


def tables(length):
    positions = jnp.arange(length, dtype=jnp.int32)
    wrapped = positions[:, None] * positions[None, :] % length
    angles = wrapped.astype(jnp.float32) * (2.0 * math.pi / length)
    return (jnp.cos(angles), jnp.sin(angles))


def contract(pattern, left_operand, right_operand):
    return jnp.einsum(pattern, left_operand, right_operand, precision=highest)


def rotate(pattern, real_part, imag_part, cosine_table, sine_table, orient):
    new_real = contract(pattern, real_part, cosine_table) - orient * contract(
        pattern, imag_part, sine_table
    )
    new_imag = contract(pattern, imag_part, cosine_table) + orient * contract(
        pattern, real_part, sine_table
    )
    return (new_real, new_imag)


def rotate_real(pattern, real_part, cosine_table, sine_table, orient):
    return (
        contract(pattern, real_part, cosine_table),
        orient * contract(pattern, real_part, sine_table),
    )


def frequency(length, offset, extent):
    positions = offset + jnp.arange(extent, dtype=jnp.int32)
    signed = jnp.where(2 * positions < length, positions, positions - length)
    return signed.astype(jnp.float32)


def coulomb(first_freq, second_freq, third_freq):
    squared = (
        first_freq[:, None, None] ** 2
        + second_freq[None, :, None] ** 2
        + third_freq[None, None, :] ** 2
    )
    scaled = box_length**2 / math.pi / jnp.maximum(squared, 1.0)
    return jnp.where(squared > 0, scaled, 0.0)


def potential_split(density_share, cosine_table, sine_table, length):
    real_part, imag_part = rotate_real(
        "kxyz,zg->kxgy", density_share, cosine_table, sine_table, -1.0
    )
    arrived = lax.all_to_all(
        jnp.stack((real_part, imag_part)), "band", split_axis=3, concat_axis=4, tiled=True
    )
    real_part, imag_part = rotate(
        "kxzy,yg->kgzx", arrived[0], arrived[1], cosine_table, sine_table, -1.0
    )
    arrived = lax.all_to_all(
        jnp.stack((real_part, imag_part)), "grid", split_axis=2, concat_axis=4, tiled=True
    )
    real_part, imag_part = rotate(
        "kyzx,xg->kyzg", arrived[0], arrived[1], cosine_table, sine_table, -1.0
    )
    rows_here = real_part.shape[1]
    planes_here = real_part.shape[2]
    kernel = coulomb(
        frequency(length, lax.axis_index("grid") * rows_here, rows_here),
        frequency(length, lax.axis_index("band") * planes_here, planes_here),
        frequency(length, 0, length),
    )
    real_part = real_part * kernel[None]
    imag_part = imag_part * kernel[None]
    real_part, imag_part = rotate(
        "kyzg,gx->kyzx", real_part, imag_part, cosine_table, sine_table, 1.0
    )
    arrived = lax.all_to_all(
        jnp.stack((real_part, imag_part)), "grid", split_axis=4, concat_axis=2, tiled=True
    )
    real_part, imag_part = rotate(
        "kgzx,gy->kxzy", arrived[0], arrived[1], cosine_table, sine_table, 1.0
    )
    arrived = lax.all_to_all(
        jnp.stack((real_part, imag_part)), "band", split_axis=4, concat_axis=3, tiled=True
    )
    restored = contract("kxgy,gz->kxyz", arrived[0], cosine_table) - contract(
        "kxgy,gz->kxyz", arrived[1], sine_table
    )
    return restored / float(length**3)


def per_device(orbitals, trial_vectors, alda_kernel, local_potential, band_energies):
    length = orbitals.shape[2]
    cosine_table, sine_table = tables(length)
    orbital_wide = orbitals.astype(jnp.float32)
    trial_wide = trial_vectors.astype(jnp.float32)
    partial_value = 2.0 * jnp.sum(trial_wide * orbital_wide[None], axis=1)
    density_share = lax.psum_scatter(partial_value, "band", scatter_dimension=2, tiled=True)
    row_count = density_share.shape[2]
    kernel_rows = lax.dynamic_slice_in_dim(
        alda_kernel, lax.axis_index("band") * row_count, row_count, 1
    )
    hartree = potential_split(density_share, cosine_table, sine_table, length)
    potential = lax.all_gather(
        hartree + kernel_rows[None] * density_share, "band", axis=2, tiled=True
    )
    weight = local_potential[None] - band_energies[:, None, None, None]
    fields = potential[:, None] * orbital_wide[None] + weight[None] * trial_wide
    trial_count = trial_vectors.shape[0]
    norm_factor = float(length) ** (-1.5)
    pieces = []
    for trial_index in range(trial_count):
        real_part, imag_part = rotate_real(
            "mxyz,zg->mxyg", fields[trial_index], cosine_table, sine_table, -1.0
        )
        real_part, imag_part = rotate(
            "mxyz,yg->mgzx", real_part, imag_part, cosine_table, sine_table, -1.0
        )
        received = lax.all_to_all(
            jnp.stack((real_part, imag_part)), "grid", split_axis=2, concat_axis=4, tiled=True
        )
        finish_real_part, finish_imag_part = rotate(
            "myzx,xg->myzg", received[0], received[1], cosine_table, sine_table, -1.0
        )
        pieces.append(jnp.stack((finish_real_part * norm_factor, finish_imag_part * norm_factor)))
    results = jnp.stack(pieces, axis=1)
    return (results[0], results[1])


def solution(mesh):
    placed = (
        P("band", "grid", None, None),
        P(None, "band", "grid", None, None),
        P("grid", None, None),
        P("grid", None, None),
        P("band"),
    )
    return jax.shard_map(
        per_device,
        mesh=mesh,
        in_specs=placed,
        out_specs=(P(None, "band", "grid", None, None), P(None, "band", "grid", None, None)),
        check_vma=False,
    )
```

profile of v0, /device:TPU:0, one launch (start us, length us, event | category | flops | bytes accessed | tf_op | source)
XLA Modules:
  0.0 582.9 jit_solution(3529673383581125716)
XLA Ops:
  10.2 2.7 fusion.1
  13.0 91.5 %reduce-scatter.2.cloned.1.call-done = f32[2,32,16,128]{3,2,1,0:T(8,128)} async-done(((f32[2,32,128,128]{3,2,1,0:T(8,128)}), f32[2,32,16,128]{3,2,1,0:T(8,128)}) %reduce-scatter.2.cloned.1.call-update) | async-done | bytes 524304 | tf_op jit(solution)/shard_map/reduce_scatter | solution.py:104
  108.4 4.4 copy.166
  112.8 4.8 reshape.245
  117.6 4.6 all-to-all-start
  122.2 25.6 %all-to-all-done = f32[8,1,32768]{2,1,0:T(1,128)S(1)} async-done(((f32[8,1,32768]{2,1,0:T(1,128)}), f32[8,1,32768]{2,1,0:T(1,128)S(1)}, u32[]{:S(2)}, u32[]{:S(2)}) %all-to-all-start) | async-done | bytes 1048608 | tf_op jit(solution)/shard_map/all_to_all | solution.py:59
  149.4 4.3 reduce
  153.7 3.4 reshape.246
  157.1 2.6 copy.167
  160.4 3.5 convolution_multiply_fusion.1
  164.1 3.5 convolution_multiply_fusion
  167.6 14.0 %fusion.27 = f32[1,2,128,16,32]{2,4,3,1,0:T(8,128)S(1)} fusion(f32[128,2,32,16]{0,2,3,1:T(8,128)S(1)} %convolution_multiply_fusion.1, f32[2,32,16,128]{1,3,2,0:T(8,128)S(1)} %bitcast.275), kind=kOutput, calls=%fused_computation.44 | convolution fusion | flops 201687040 | bytes 1572864 | tf_op jit(solution)/shard_map/kxzy,yg->kgzx/dot_general | solution.py:19
  181.6 3.5 fusion.26
  185.1 4.4 copy.174
  189.5 4.8 reshape.247
  194.4 4.2 all-to-all-start.1
  198.9 14.2 %all-to-all-done.1 = f32[4,1,65536]{2,1,0:T(1,128)} async-done(((f32[4,1,65536]{2,1,0:T(1,128)}), f32[4,1,65536]{2,1,0:T(1,128)}, u32[]{:S(2)}, u32[]{:S(2)}) %all-to-all-start.1) | async-done | bytes 1048608 | tf_op jit(solution)/shard_map/all_to_all | solution.py:65
  213.1 4.6 reduce.1
  217.7 3.5 reshape.248
  221.2 4.9 copy.248
  226.0 2.3 fusion.316
  228.4 2.4 squeeze.38
  230.8 2.8 squeeze.39
  240.4 4.4 copy.176
  244.8 3.9 reshape.249
  248.7 17.7 %all_to_all.90 = f32[4,1,65536]{2,1,0:T(1,128)} all-to-all(f32[4,1,65536]{2,1,0:T(1,128)S(1)} %reshape.249), channel_id=1, replica_groups=mesh['band'=8,'grid'=4] {'grid'}, dimensions={0} | all-to-all | bytes 2097152 | tf_op jit(solution)/shard_map/all_to_all | solution.py:83
  266.4 4.6 reduce.2
  271.0 3.5 reshape.250
  274.5 4.9 copy.247
  279.4 2.3 fusion.315
  281.6 2.4 squeeze.40
  286.5 2.4 squeeze.41
  290.9 4.4 copy.178
  295.3 4.8 reshape.251
  300.2 3.6 all-to-all-start.3
  304.3 25.1 %all-to-all-done.3 = f32[8,1,32768]{2,1,0:T(1,128)S(1)} async-done(((f32[8,1,32768]{2,1,0:T(1,128)}), f32[8,1,32768]{2,1,0:T(1,128)S(1)}, u32[]{:S(2)}, u32[]{:S(2)}) %all-to-all-start.3) | async-done | bytes 1048608 | tf_op jit(solution)/shard_map/all_to_all | solution.py:89
  329.4 3.1 reduce.3
  332.5 3.4 reshape.252
  335.9 4.6 copy.179
  347.7 2.7 fusion.29
  351.1 3.3 broadcast_subtract_fusion
  354.4 69.1 %all-gather.2.cloned.1.call-done = f32[2,32,128,128]{3,2,1,0:T(8,128)} async-done(((f32[2,32,16,128]{3,2,1,0:T(8,128)}), f32[2,32,128,128]{3,2,1,0:T(8,128)}) %all-gather.2.cloned.1.call-update) | async-done | bytes 4194320 | tf_op jit(solution)/shard_map/all_gather | solution.py:110
  423.5 4.7 fusion.2
  436.8 2.3 subtract_bitcast_fusion.1
  439.1 2.7 add_bitcast_fusion.1
  442.3 4.4 copy.188
  446.7 4.8 all-to-all-start.4
  451.6 3.8 fusion.8
  464.2 2.5 add_bitcast_fusion
  467.1 4.4 copy.201
  471.6 28.2 %all-to-all-done.4 = f32[2,1,128,128,32]{3,4,1,0,2:T(8,128)} async-done(((f32[2,1,128,128,32]{3,4,1,0,2:T(8,128)}), f32[2,1,128,128,32]{3,4,1,0,2:T(8,128)}, u32[]{:S(2)}, u32[]{:S(2)}) %all-to-all-start.4) | async-done | bytes 4194336 | tf_op jit(solution)/shard_map/all_to_all | solution.py:125
  499.8 4.9 all-to-all-start.5
  504.6 2.7 copy.189
  508.3 3.6 fusion.92
  511.9 5.0 multiply_bitcast_fusion.3
  517.0 4.0 fusion.90
  521.0 4.9 multiply_bitcast_fusion.2
  525.9 26.9 %all-to-all-done.5 = f32[2,1,128,128,32]{3,4,1,0,2:T(8,128)} async-done(((f32[2,1,128,128,32]{3,4,1,0,2:T(8,128)}), f32[2,1,128,128,32]{3,4,1,0,2:T(8,128)}, u32[]{:S(2)}, u32[]{:S(2)}) %all-to-all-start.5) | async-done | bytes 4194336 | tf_op jit(solution)/shard_map/all_to_all | solution.py:125
  552.8 2.7 copy.202
  556.3 3.6 fusion.87
  560.1 3.8 fusion.85
  563.9 3.7 multiply_bitcast_fusion.1
  567.6 3.6 multiply_bitcast_fusion
  572.2 3.6 fusion.5
  (82 shorter events, 49.3 us)
Async XLA Ops:
  7.2 297.1 %copy-start = (f32[32,128,128]{2,1,0:T(8,128)S(1)}, f32[32,128,128]{2,1,0:T(8,128)}, u32[]{:S(2)}) copy-start(f32[32,128,128]{2,1,0:T(8,128)} %param.7) | copy-start | bytes 6291460
  7.2 97.3 %reduce-scatter.2.cloned.1.call-start = ((), (), s32[]{:S(2)}) async-start(), calls=%async_computation.7 | async-start | bytes 4718592 | tf_op jit(solution)/shard_map/reduce_scatter | solution.py:104
  7.2 3.0 copy-start.6
  8.9 1.4 copy-start.4
  117.6 30.2 %all-to-all-start = ((f32[8,1,32768]{2,1,0:T(1,128)}), f32[8,1,32768]{2,1,0:T(1,128)S(1)}, u32[]{:S(2)}, u32[]{:S(2)}) async-start(f32[8,1,32768]{2,1,0:T(1,128)} %reshape.245), calls=%async_computation.1 | async-start | bytes 2097152 | tf_op jit(solution)/shard_map/all_to_all | solution.py:59
  147.9 1.0 copy-start.10
  194.4 18.7 %all-to-all-start.1 = ((f32[4,1,65536]{2,1,0:T(1,128)}), f32[4,1,65536]{2,1,0:T(1,128)}, u32[]{:S(2)}, u32[]{:S(2)}) async-start(f32[4,1,65536]{2,1,0:T(1,128)} %reshape.247), calls=%async_computation.2 | async-start | bytes 2097152 | tf_op jit(solution)/shard_map/all_to_all | solution.py:65
  289.0 1.7 copy-start.11
  300.2 29.2 %all-to-all-start.3 = ((f32[8,1,32768]{2,1,0:T(1,128)}), f32[8,1,32768]{2,1,0:T(1,128)S(1)}, u32[]{:S(2)}, u32[]{:S(2)}) async-start(f32[8,1,32768]{2,1,0:T(1,128)} %reshape.251), calls=%async_computation.4 | async-start | bytes 2097152 | tf_op jit(solution)/shard_map/all_to_all | solution.py:89
  303.8 119.7 %all-gather.2.cloned.1.call-start = ((), (), s32[]{:S(2)}) async-start(), calls=%async_computation.8 | async-start | bytes 4718592 | tf_op jit(solution)/shard_map/all_gather | solution.py:110
  346.0 1.7 copy-start.9
  351.1 72.4 %copy-start.5 = (f32[32,128,128]{2,1,0:T(8,128)S(1)}, f32[32,128,128]{2,1,0:T(8,128)}, u32[]{:S(2)}) copy-start(f32[32,128,128]{2,1,0:T(8,128)} %copy-done.4) | copy-start | bytes 6291460
  428.2 2.1 copy-start.2
  446.7 53.1 %all-to-all-start.4 = ((f32[2,1,128,128,32]{3,4,1,0,2:T(8,128)}), f32[2,1,128,128,32]{3,4,1,0,2:T(8,128)}, u32[]{:S(2)}, u32[]{:S(2)}) async-start(f32[2,1,128,128,32]{3,4,1,0,2:T(8,128)} %copy.188), calls=%async_computation.5 | async-start | bytes 8388608 | tf_op jit(solution)/shard_map/all_to_all | solution.py:125
  451.6 3.8 copy-start.3
  499.8 53.1 %all-to-all-start.5 = ((f32[2,1,128,128,32]{3,4,1,0,2:T(8,128)}), f32[2,1,128,128,32]{3,4,1,0,2:T(8,128)}, u32[]{:S(2)}, u32[]{:S(2)}) async-start(f32[2,1,128,128,32]{3,4,1,0,2:T(8,128)} %copy.201), calls=%async_computation.6 | async-start | bytes 8388608 | tf_op jit(solution)/shard_map/all_to_all | solution.py:125
  567.6 3.6 copy-start.7
  567.6 3.6 copy-start.8
  572.2 3.6 copy-start.1
Sparse Core Ops, SparseCore 0:
  13.1 91.3 reduce-scatter.1
  350.5 72.9 all-gather.1
where the time goes:
time: 588 us; the launch traced here: 583 us
  waiting for transfers between devices  281 us (48%)
  local copies, waits for them, and re-layouts  108 us (18%)
  matrix products  103 us (18%)
  other arithmetic  35.2 us (6%)
  starting transfers between devices  22.7 us (4%)
  blocking collectives  17.7 us (3%)
  between operations  15.6 us (3%)
    dot_general x36, matrix products, contract(): return jnp.einsum(pattern, left_operand, right_operand, precision=highest)  99 us
    reduce_scatter x1, waiting for transfers between devices, per_device(): lax.psum_scatter(partial_value, 'band', scatter_dimension=2, tiled=True)  91.5 us
    all_gather x1, waiting for transfers between devices, per_device(): lax.all_gather(hartree + kernel_rows[None] * density_share, 'band', axis=...  69.1 us
    all_to_all x2, waiting for transfers between devices, per_device(): lax.all_to_all(jnp.stack((real_part, imag_part)), 'grid', split_axis=2, c...  55.1 us
    unnamed x32, local copies, waits for them, and re-layouts  34.5 us
    all_to_all x1, waiting for transfers between devices, potential_split(): lax.all_to_all(jnp.stack((real_part, imag_part)), 'band', split_axis=3, c...  25.6 us
    all_to_all x1, waiting for transfers between devices, potential_split(): lax.all_to_all(jnp.stack((real_part, imag_part)), 'band', split_axis=4, c...  25.1 us
    all_to_all x1, blocking collectives, potential_split(): lax.all_to_all(jnp.stack((real_part, imag_part)), 'grid', split_axis=4, c...  17.7 us
  transfers between devices with their start and end apart: 7, of which 7 were waited for; matrix products, arithmetic and copies ran while one was open for 8% of the time, Pallas kernels for 0%

commit v1 on v0

--- a/solution.py
+++ b/solution.py
@@ -107,9 +107,15 @@
         alda_kernel, lax.axis_index("band") * row_count, row_count, 1
     )
     hartree = potential_split(density_share, cosine_table, sine_table, length)
-    potential = lax.all_gather(
-        hartree + kernel_rows[None] * density_share, "band", axis=2, tiled=True
-    )
+    x = hartree + kernel_rows[None] * density_share
+    ways, here = (lax.axis_size("band"), lax.axis_index("band"))
+    potential, reach = (x, 1)
+    while reach < ways:
+        theirs = lax.ppermute(potential, "band", [(d, d ^ reach) for d in range(ways)])
+        mine_first = jnp.concatenate([potential, theirs], axis=2)
+        theirs_first = jnp.concatenate([theirs, potential], axis=2)
+        potential = jnp.where(here & reach == 0, mine_first, theirs_first)
+        reach = 2 * reach
     weight = local_potential[None] - band_energies[:, None, None, None]
     fields = potential[:, None] * orbital_wide[None] + weight[None] * trial_wide
     trial_count = trial_vectors.shape[0]

time: 588 us -> 644 us (1.095)
  waiting for transfers between devices: 281 us -> 333 us
    ppermute x0 -> x3, waiting for transfers between devices: none -> 121 us  [per_device(): lax.ppermute(potential, 'band', [(d, d ^ reach) for d in range(ways)])]
    all_gather x1 -> x0, waiting for transfers between devices: 69.1 us -> none  [per_device(): lax.all_gather(hartree + kernel_rows[None] * density_share, 'band', axis=...]
    unnamed x32 -> x34, local copies, waits for them, and re-layouts: 34.5 us -> 34.5 us
  transfers between devices with their start and end apart: 7 -> 9, of which waited for: 7 -> 9; matrix products, arithmetic and copies ran while one was open for 8% -> 7% of each run, Pallas kernels for 0% -> 0%
where the time goes in v1:
time: 644 us; the launch traced here: 639 us
  waiting for transfers between devices  333 us (52%)
  local copies, waits for them, and re-layouts  108 us (17%)
  matrix products  102 us (16%)
  other arithmetic  35.6 us (6%)
  starting transfers between devices  26.6 us (4%)
  blocking collectives  17.8 us (3%)
  between operations  15.7 us (2%)
    ppermute x3, waiting for transfers between devices, per_device(): lax.ppermute(potential, 'band', [(d, d ^ reach) for d in range(ways)])  121 us
    dot_general x36, matrix products, contract(): return jnp.einsum(pattern, left_operand, right_operand, precision=highest)  98.2 us
    reduce_scatter x1, waiting for transfers between devices, per_device(): lax.psum_scatter(partial_value, 'band', scatter_dimension=2, tiled=True)  91.5 us
    all_to_all x2, waiting for transfers between devices, per_device(): lax.all_to_all(jnp.stack((real_part, imag_part)), 'grid', split_axis=2, c...  55.1 us
    unnamed x34, local copies, waits for them, and re-layouts  34.5 us
    all_to_all x1, waiting for transfers between devices, potential_split(): lax.all_to_all(jnp.stack((real_part, imag_part)), 'band', split_axis=3, c...  25.6 us
    all_to_all x1, waiting for transfers between devices, potential_split(): lax.all_to_all(jnp.stack((real_part, imag_part)), 'band', split_axis=4, c...  25.5 us
    all_to_all x1, blocking collectives, potential_split(): lax.all_to_all(jnp.stack((real_part, imag_part)), 'grid', split_axis=4, c...  17.8 us
  transfers between devices with their start and end apart: 9, of which 9 were waited for; matrix products, arithmetic and copies ran while one was open for 7% of the time, Pallas kernels for 0%

profile of v1, /device:TPU:0, one launch (start us, length us, event | category | flops | bytes accessed | tf_op | source)
XLA Modules:
  0.0 638.9 jit_solution(8089317602935812079)
XLA Ops:
  10.2 2.7 fusion.1
  13.0 91.5 %reduce-scatter.2.cloned.1.call-done = f32[2,32,16,128]{3,2,1,0:T(8,128)} async-done(((f32[2,32,128,128]{3,2,1,0:T(8,128)}), f32[2,32,16,128]{3,2,1,0:T(8,128)}) %reduce-scatter.2.cloned.1.call-update) | async-done | bytes 524304 | tf_op jit(solution)/shard_map/reduce_scatter | solution.py:104
  108.4 4.4 copy.166
  112.8 4.8 reshape.351
  117.6 4.6 all-to-all-start
  122.2 25.6 %all-to-all-done = f32[8,1,32768]{2,1,0:T(1,128)S(1)} async-done(((f32[8,1,32768]{2,1,0:T(1,128)}), f32[8,1,32768]{2,1,0:T(1,128)S(1)}, u32[]{:S(2)}, u32[]{:S(2)}) %all-to-all-start) | async-done | bytes 1048608 | tf_op jit(solution)/shard_map/all_to_all | solution.py:59
  149.4 4.3 reduce
  153.7 3.4 reshape.352
  157.1 2.6 copy.167
  160.4 3.5 convolution_multiply_fusion.1
  164.1 3.5 convolution_multiply_fusion
  167.6 14.0 %fusion.28 = f32[1,2,128,16,32]{2,4,3,1,0:T(8,128)S(1)} fusion(f32[128,2,32,16]{0,2,3,1:T(8,128)S(1)} %convolution_multiply_fusion.1, f32[2,32,16,128]{1,3,2,0:T(8,128)S(1)} %bitcast.275), kind=kOutput, calls=%fused_computation.47 | convolution fusion | flops 201687040 | bytes 1572864 | tf_op jit(solution)/shard_map/kxzy,yg->kgzx/dot_general | solution.py:19
  181.6 3.5 fusion.27
  185.2 4.4 copy.174
  189.6 4.8 reshape.353
  194.4 4.3 all-to-all-start.1
  198.9 14.2 %all-to-all-done.1 = f32[4,1,65536]{2,1,0:T(1,128)} async-done(((f32[4,1,65536]{2,1,0:T(1,128)}), f32[4,1,65536]{2,1,0:T(1,128)}, u32[]{:S(2)}, u32[]{:S(2)}) %all-to-all-start.1) | async-done | bytes 1048608 | tf_op jit(solution)/shard_map/all_to_all | solution.py:65
  213.2 4.6 reduce.1
  217.7 3.5 reshape.354
  221.2 4.9 copy.248
  226.1 2.3 fusion.317
  228.4 2.4 squeeze.38
  230.9 2.8 squeeze.39
  240.4 4.4 copy.176
  244.8 3.9 reshape.355
  248.7 17.8 %all_to_all.90 = f32[4,1,65536]{2,1,0:T(1,128)} all-to-all(f32[4,1,65536]{2,1,0:T(1,128)S(1)} %reshape.355), channel_id=1, replica_groups=mesh['band'=8,'grid'=4] {'grid'}, dimensions={0} | all-to-all | bytes 2097152 | tf_op jit(solution)/shard_map/all_to_all | solution.py:83
  266.5 4.6 reduce.2
  271.1 3.5 reshape.356
  274.5 4.9 copy.247
  279.4 2.3 fusion.316
  281.7 2.4 squeeze.40
  286.6 2.4 squeeze.41
  291.0 4.4 copy.178
  295.4 4.8 reshape.357
  300.3 4.1 all-to-all-start.3
  304.4 25.5 %all-to-all-done.3 = f32[8,1,32768]{2,1,0:T(1,128)S(1)} async-done(((f32[8,1,32768]{2,1,0:T(1,128)}), f32[8,1,32768]{2,1,0:T(1,128)S(1)}, u32[]{:S(2)}, u32[]{:S(2)}) %all-to-all-start.3) | async-done | bytes 1048608 | tf_op jit(solution)/shard_map/all_to_all | solution.py:89
  329.9 3.1 reduce.3
  333.0 3.4 reshape.358
  336.4 4.6 copy.179
  351.5 11.2 %collective-permute-done = f32[2,32,16,128]{3,2,1,0:T(8,128)S(1)} collective-permute-done((f32[2,32,16,128]{3,2,1,0:T(8,128)S(1)}, f32[2,32,16,128]{3,2,1,0:T(8,128)S(1)}, u32[]{:S(2)}, u32[]{:S(2)}) %collective-permute-start) | collective-permute-done | bytes 524320 | tf_op jit(solution)/shard_map/ppermute | solution.py:114
  363.0 22.9 %collective-permute-done.1 = f32[2,32,32,128]{3,2,1,0:T(8,128)S(1)} collective-permute-done((f32[2,32,32,128]{3,2,1,0:T(8,128)S(1)}, f32[2,32,32,128]{3,2,1,0:T(8,128)S(1)}, u32[]{:S(2)}, u32[]{:S(2)}) %collective-permute-start.1) | collective-permute-done | bytes 1048608 | tf_op jit(solution)/shard_map/ppermute | solution.py:114
  387.6 2.4 collective-permute-start.2
  392.6 87.0 %collective-permute-done.2 = f32[2,32,64,128]{3,2,1,0:T(8,128)} collective-permute-done((f32[2,32,64,128]{3,2,1,0:T(8,128)}, f32[2,32,64,128]{3,2,1,0:T(8,128)}, u32[]{:S(2)}, u32[]{:S(2)}) %collective-permute-start.2) | collective-permute-done | bytes 2097184 | tf_op jit(solution)/shard_map/ppermute | solution.py:114
  479.6 4.6 fusion.2
  495.1 2.7 add_bitcast_fusion.1
  498.3 4.4 copy.188
  502.7 4.9 all-to-all-start.4
  507.6 3.8 fusion.9
  520.2 2.5 add_bitcast_fusion
  523.1 4.4 copy.201
  527.6 28.2 %all-to-all-done.4 = f32[2,1,128,128,32]{3,4,1,0,2:T(8,128)} async-done(((f32[2,1,128,128,32]{3,4,1,0,2:T(8,128)}), f32[2,1,128,128,32]{3,4,1,0,2:T(8,128)}, u32[]{:S(2)}, u32[]{:S(2)}) %all-to-all-start.4) | async-done | bytes 4194336 | tf_op jit(solution)/shard_map/all_to_all | solution.py:131
  555.8 4.9 all-to-all-start.5
  560.6 2.7 copy.189
  564.3 3.6 fusion.93
  567.9 5.0 multiply_bitcast_fusion.3
  573.0 4.0 fusion.91
  577.0 4.9 multiply_bitcast_fusion.2
  581.9 27.0 %all-to-all-done.5 = f32[2,1,128,128,32]{3,4,1,0,2:T(8,128)} async-done(((f32[2,1,128,128,32]{3,4,1,0,2:T(8,128)}), f32[2,1,128,128,32]{3,4,1,0,2:T(8,128)}, u32[]{:S(2)}, u32[]{:S(2)}) %all-to-all-start.5) | async-done | bytes 4194336 | tf_op jit(solution)/shard_map/all_to_all | solution.py:131
  608.8 2.7 copy.202
  612.3 3.6 fusion.88
  616.1 3.8 fusion.86
  619.9 3.7 multiply_bitcast_fusion.1
  623.6 3.6 multiply_bitcast_fusion
  628.3 3.6 fusion.5
  (89 shorter events, 58.3 us)
Async XLA Ops:
  7.2 297.2 %copy-start = (f32[32,128,128]{2,1,0:T(8,128)S(1)}, f32[32,128,128]{2,1,0:T(8,128)}, u32[]{:S(2)}) copy-start(f32[32,128,128]{2,1,0:T(8,128)} %param.7) | copy-start | bytes 6291460
  7.2 97.3 %reduce-scatter.2.cloned.1.call-start = ((), (), s32[]{:S(2)}) async-start(), calls=%async_computation.7 | async-start | bytes 4718592 | tf_op jit(solution)/shard_map/reduce_scatter | solution.py:104
  7.2 3.0 copy-start.8
  8.9 1.3 copy-start.4
  117.6 30.2 %all-to-all-start = ((f32[8,1,32768]{2,1,0:T(1,128)}), f32[8,1,32768]{2,1,0:T(1,128)S(1)}, u32[]{:S(2)}, u32[]{:S(2)}) async-start(f32[8,1,32768]{2,1,0:T(1,128)} %reshape.351), calls=%async_computation.1 | async-start | bytes 2097152 | tf_op jit(solution)/shard_map/all_to_all | solution.py:59
  147.8 1.0 copy-start.11
  194.4 18.8 %all-to-all-start.1 = ((f32[4,1,65536]{2,1,0:T(1,128)}), f32[4,1,65536]{2,1,0:T(1,128)}, u32[]{:S(2)}, u32[]{:S(2)}) async-start(f32[4,1,65536]{2,1,0:T(1,128)} %reshape.353), calls=%async_computation.2 | async-start | bytes 2097152 | tf_op jit(solution)/shard_map/all_to_all | solution.py:65
  289.0 1.7 copy-start.12
  300.3 29.6 %all-to-all-start.3 = ((f32[8,1,32768]{2,1,0:T(1,128)}), f32[8,1,32768]{2,1,0:T(1,128)S(1)}, u32[]{:S(2)}, u32[]{:S(2)}) async-start(f32[8,1,32768]{2,1,0:T(1,128)} %reshape.357), calls=%async_computation.4 | async-start | bytes 2097152 | tf_op jit(solution)/shard_map/all_to_all | solution.py:89
  346.4 1.8 copy-start.10
  350.1 12.6 %collective-permute-start = (f32[2,32,16,128]{3,2,1,0:T(8,128)S(1)}, f32[2,32,16,128]{3,2,1,0:T(8,128)S(1)}, u32[]{:S(2)}, u32[]{:S(2)}) collective-permute-start(f32[2,32,16,128]{3,2,1,0:T(8,128)S(1)} %fusion.30), channel_id=1, source_target_pairs={{0,4},{4,0},{8,12},{12,8},{16,20},{20,16},{24,28},{28,24},{1,5},{5... | collective-permute-start | bytes 1572872 | tf_op jit(solution)/shard_map/ppermute | solution.py:114
  362.9 23.0 %collective-permute-start.1 = (f32[2,32,32,128]{3,2,1,0:T(8,128)S(1)}, f32[2,32,32,128]{3,2,1,0:T(8,128)S(1)}, u32[]{:S(2)}, u32[]{:S(2)}) collective-permute-start(f32[2,32,32,128]{3,2,1,0:T(8,128)S(1)} %maximum_select_fusion.2), channel_id=1, source_target_pairs={{0,8},{4,12},{8,0},{12,4},{16,24},{20,28},{24,16},{28,20},{1,9},{5... | collective-permute-start | bytes 3145736 | tf_op jit(solution)/shard_map/ppermute | solution.py:114
  387.6 92.0 %collective-permute-start.2 = (f32[2,32,64,128]{3,2,1,0:T(8,128)}, f32[2,32,64,128]{3,2,1,0:T(8,128)}, u32[]{:S(2)}, u32[]{:S(2)}) collective-permute-start(f32[2,32,64,128]{3,2,1,0:T(8,128)} %maximum_select_fusion.1), channel_id=1, source_target_pairs={{0,16},{4,20},{8,24},{12,28},{16,0},{20,4},{24,8},{28,12},{1,17},{... | collective-permute-start | bytes 6291464 | tf_op jit(solution)/shard_map/ppermute | solution.py:114
  390.7 88.9 %copy-start.5 = (f32[32,128,128]{2,1,0:T(8,128)S(1)}, f32[32,128,128]{2,1,0:T(8,128)}, u32[]{:S(2)}) copy-start(f32[32,128,128]{2,1,0:T(8,128)} %copy-done.4) | copy-start | bytes 6291460
  390.7 88.9 %copy-start.9 = (bf16[2,1,32,128,128]{4,3,2,1,0:T(8,128)(2,1)S(1)}, bf16[2,1,32,128,128]{4,3,2,1,0:T(8,128)(2,1)}, u32[]{:S(2)}) copy-start(bf16[2,1,32,128,128]{4,3,2,1,0:T(8,128)(2,1)} %param.6) | copy-start | bytes 6291460
  484.2 2.1 copy-start.2
  502.7 53.1 %all-to-all-start.4 = ((f32[2,1,128,128,32]{3,4,1,0,2:T(8,128)}), f32[2,1,128,128,32]{3,4,1,0,2:T(8,128)}, u32[]{:S(2)}, u32[]{:S(2)}) async-start(f32[2,1,128,128,32]{3,4,1,0,2:T(8,128)} %copy.188), calls=%async_computation.5 | async-start | bytes 8388608 | tf_op jit(solution)/shard_map/all_to_all | solution.py:131
  507.6 3.8 copy-start.3
  555.8 53.1 %all-to-all-start.5 = ((f32[2,1,128,128,32]{3,4,1,0,2:T(8,128)}), f32[2,1,128,128,32]{3,4,1,0,2:T(8,128)}, u32[]{:S(2)}, u32[]{:S(2)}) async-start(f32[2,1,128,128,32]{3,4,1,0,2:T(8,128)} %copy.201), calls=%async_computation.6 | async-start | bytes 8388608 | tf_op jit(solution)/shard_map/all_to_all | solution.py:131
  623.6 3.6 copy-start.6
  623.6 3.6 copy-start.7
  628.3 3.6 copy-start.1
Sparse Core Ops, SparseCore 0:
  13.1 91.3 reduce-scatter.1
